TPU v7x, 32 devices: a whole 2x2x4 slice. The times are simulated.
32 devices in a mesh: cls: 4 (over y, x), dom: 8 (over z, core).
Axes of the slice: x: 2, y: 2, z: 4, core: 2. Of those that a mesh axis runs over, the one named last changes fastest.
Arguments:
- particles: bfloat16 [256, 2, 110592], P(('cls', 'dom')), may hold values from -18 to 18
- labels: int32 [256, 1], P(('cls', 'dom')), may hold values from 0 to 7; in each aligned block of 8 rows (0 to 7, 8 to 15, ...) at most 2 rows name the same one
- wedge_index: int32 [256], P(('cls', 'dom')), may hold values from 0 to 11
- wedge_table: float32 [12, 110592], replicated, may hold values from 0.05 to 1
Outputs:
- class_average: float32 [8, 2, 110592], P('cls', None, 'dom')
- weight_total: float32 [8, 110592], P('cls', 'dom')
Inputs may be any that keep to these rules, and one draw needn't show every extreme that they name: `labels`: among the rows of one device no class appears more than 2 times, and on some devices one class appears exactly 2 times; every class appears on some device.
All inputs are finite; a program needn't handle non-finite values.
Results may differ from a plain program's by a relative error of at most 0.0003.
Values may be sent and summed in bfloat16 or wider, within the bound.
A program may use at most 128 MiB of HBM per device.

v0:
```python
import jax
import jax.numpy as jnp
from jax import lax
from jax.sharding import PartitionSpec as P

CLS_GROUP = 2


def per_device(particles, labels, wedge_index, wedge_table):
    n_cls = lax.axis_size("cls")
    n_dom = lax.axis_size("dom")
    p_dev = particles.shape[0]
    voxels = particles.shape[2]
    shard_len = voxels // n_dom
    wedge_count = wedge_table.shape[0]
    label_flat = labels[:, 0]
    parts_four = particles.reshape(p_dev, 2, n_dom, shard_len)
    dom_pos = lax.axis_index("dom")
    table_shard = lax.dynamic_slice_in_dim(wedge_table, dom_pos * shard_len, shard_len, 1)
    got_data = lax.all_to_all(parts_four, "dom", split_axis=2, concat_axis=0, tiled=True)
    got_data = got_data.reshape(n_dom * p_dev, 2, shard_len)
    group_labels, group_wedges = (
        lax.all_gather(label_flat, "dom", axis=0, tiled=True),
        lax.all_gather(wedge_index, "dom", axis=0, tiled=True),
    )
    pick = (group_wedges[:, None] == jnp.arange(wedge_count, dtype=jnp.int32)[None, :]).astype(
        jnp.float32
    )
    weight = jnp.dot(pick, table_shard, precision=lax.Precision.HIGHEST)
    member = (
        jnp.arange(n_cls * CLS_GROUP, dtype=jnp.int32)[:, None] == group_labels[None, :]
    ).astype(jnp.float32)
    weighted = weight[:, None, :] * got_data
    local_sums = jnp.einsum("kp,pcv->kcv", member, weighted, precision=lax.Precision.HIGHEST)
    local_totals = jnp.dot(member, weight * weight, precision=lax.Precision.HIGHEST)
    local_sums = local_sums.reshape(n_cls, CLS_GROUP, 2, shard_len)
    local_totals = local_totals.reshape(n_cls, CLS_GROUP, shard_len)
    summed, totals = (
        lax.psum_scatter(local_sums, "cls", scatter_dimension=0, tiled=True),
        lax.psum_scatter(local_totals, "cls", scatter_dimension=0, tiled=True),
    )
    weighted_sum = summed[0]
    weight_total = totals[0]
    class_average = weighted_sum / (weight_total[:, None, :] + 1.0)
    return (class_average, weight_total)


def solution(mesh):
    return jax.shard_map(
        per_device,
        mesh=mesh,
        in_specs=(P(("cls", "dom"), None, None), P(("cls", "dom"), None), P(("cls", "dom")), P()),
        out_specs=(P("cls", None, "dom"), P("cls", "dom")),
        check_vma=False,
    )
```

profile of v0, /device:TPU:0, one launch (start us, length us, event | category | flops | bytes accessed | tf_op | source)
XLA Modules:
  0.0 185.2 jit_solution(2166439948641008769)
XLA Ops:
  7.2 0.0 copy-start.3
  7.2 0.0 copy-start
  7.2 0.0 copy-start.1
  7.2 6.2 %copy.23 = bf16[8,1,8,2,13824]{4,3,1,0,2:T(2,128)(2,1)} copy(bf16[8,1,8,2,13824]{4,3,2,1,0:T(2,128)(2,1)} %bitcast.34) | data formatting | bytes 7077888 | tf_op jit(solution)/shard_map/reshape | solution.py:17
  13.4 6.4 %all-to-all-start = ((bf16[8,2,8,13824]{3,1,0,2:T(2,128)(2,1)}), bf16[8,2,8,13824]{3,1,0,2:T(2,128)(2,1)}, u32[]{:S(2)}, u32[]{:S(2)}) async-start(bf16[8,2,8,13824]{3,1,0,2:T(2,128)(2,1)} %bitcast.31), calls=%async_computation | async-start | bytes 7077888 | tf_op jit(solution)/shard_map/all_to_all | solution.py:20
  19.8 0.0 all-reduce.8.cloned.1.call-start
  19.8 0.0 copy-done.3
  19.9 0.6 dynamic-slice
  21.1 0.0 copy-done
  21.1 0.2 dynamic-update-slice.1
  21.4 0.0 copy-done.1
  21.4 0.1 bitcast_dynamic-update-slice_fusion
  21.4 78.5 %all-reduce.4 = (s32[64]{0:T(128)S(1)}, s32[64]{0:T(128)S(1)}) all-reduce(s32[64]{0:T(128)S(1)} %dynamic-update-slice.1, s32[64]{0:T(128)S(1)} %bitcast_dynamic-update-slice_fusion), channel_id=1, replica_groups=mesh['cls'=4,'dom'=8] {'dom'}, use_global_device_ids=true, to_apply=%add.1 | all-reduce | flops 128 | bytes 1024
  100.0 2.7 %fusion.6 = f32[64,13824]{1,0:T(8,128)S(1)} fusion(f32[12,110592]{1,0:T(8,128)} %param.7, s32[]{:T(128)S(6)} %select_n.3, s32[64]{0:T(128)S(1)} %get-tuple-element.2), kind=kOutput, calls=%fused_computation.8 | convolution fusion | flops 127402752 | bytes 4423940 | tf_op jit(solution)/shard_map/dot_general | solution.py:29
  102.7 2.1 %fusion.4 = f32[8,13824]{1,0:T(8,128)} fusion(f32[64,13824]{1,0:T(8,128)S(1)} %fusion.6, s32[64]{0:T(128)S(1)} %get-tuple-element.3), kind=kOutput, calls=%fused_computation.6 | convolution fusion | flops 85819904 | bytes 3981568 | tf_op jit(solution)/shard_map/dot_general | solution.py:35
  104.8 2.0 %reshape.47 = f32[4,2,13824]{2,1,0:T(2,128)} reshape(f32[8,13824]{1,0:T(8,128)} %fusion.4) | data formatting | bytes 884736 | tf_op jit(solution)/shard_map/reshape | solution.py:37
  106.8 0.0 all-to-all-done
  106.8 6.4 %fusion = f32[8,8,2,1,13824]{4,2,1,0,3:T(2,128)S(1)} fusion(bf16[8,2,8,13824]{3,1,0,2:T(2,128)(2,1)} %all-to-all-done, f32[8,8,13824]{2,1,0:T(8,128)S(1)} %bitcast.32), kind=kLoop, calls=%fused_computation.1 | loop fusion | flops 3538944 | bytes 14155776 | tf_op jit(solution)/shard_map/mul | solution.py:33
  113.3 0.0 copy-start.2
  113.3 3.1 %fusion.1 = f32[4,2,2,13824]{3,0,2,1:T(4,128)S(1)} fusion(f32[64,2,13824]{2,1,0:T(2,128)S(1)} %bitcast.33, s32[64]{0:T(128)S(1)} %get-tuple-element.3, s32[4,2]{0,1:T(2,128)S(1)} %multiply_add_fusion), kind=kOutput, calls=%fused_computation.2 | convolution fusion | flops 169869824 | bytes 7962912 | tf_op jit(solution)/shard_map/kp,pcv->kcv/dot_general | solution.py:34
  116.4 1.4 copy.13
  117.7 0.0 all-reduce.8.cloned.1.call-update
  117.8 0.0 copy-done.2
  117.8 0.6 dynamic-slice.2
  118.4 55.4 %all-reduce.8.cloned.1.call-done = (f32[4,2,2,13824]{3,2,1,0:T(2,128)}, f32[4,2,13824]{2,1,0:T(2,128)}) async-done(((f32[4,2,2,13824]{3,2,1,0:T(2,128)}, f32[4,2,13824]{2,1,0:T(2,128)}), (f32[4,2,2,13824]{3,2,1,0:T(2,128)}, f32[4,2,13824]{2,1,0:T(2,128)})) %all-reduce.8.cloned.1.call-update) | async-done | bytes 1327120
  173.8 2.2 %broadcast_add_fusion = (f32[2,13824]{1,0:T(2,128)S(1)}, f32[2,13824]{1,0:T(2,128)}) fusion(f32[4,2,13824]{2,1,0:T(2,128)} %get-tuple-element.5, u32[]{:T(128)} %bitcast.13), kind=kLoop, calls=%fused_computation.13 | loop fusion | flops 27648 | bytes 331780 | tf_op jit(solution)/shard_map/add | solution.py:44
  176.0 2.3 %fusion.8 = f32[2,2,13824]{2,1,0:T(2,128)} fusion(f32[4,2,2,13824]{3,2,1,0:T(2,128)} %get-tuple-element.4, u32[]{:T(128)} %bitcast.13, f32[2,13824]{1,0:T(2,128)S(1)} %get-tuple-element.6), kind=kLoop, calls=%fused_computation.11 | loop fusion | flops 55296 | bytes 552964 | tf_op jit(solution)/shard_map/div | solution.py:44
  (3 shorter events, 0.0 us)
Async XLA Ops:
  7.2 12.7 %copy-start.3 = (u32[32]{0:T(128)S(1)}, u32[32]{0:T(128)}, u32[]{:S(2)}) copy-start(u32[32]{0:T(128)} %constant.19) | copy-start | bytes 388
  7.2 13.9 %copy-start = (s32[8]{0:T(128)S(1)}, s32[8]{0:T(128)}, u32[]{:S(2)}) copy-start(s32[8]{0:T(128)} %param.6) | copy-start | bytes 100
  7.2 14.2 %copy-start.1 = (s32[8,1]{0,1:T(1,128)S(1)}, s32[8,1]{0,1:T(1,128)}, u32[]{:S(2)}) copy-start(s32[8,1]{0,1:T(1,128)} %param.5) | copy-start | bytes 100
  13.4 93.4 %all-to-all-start = ((bf16[8,2,8,13824]{3,1,0,2:T(2,128)(2,1)}), bf16[8,2,8,13824]{3,1,0,2:T(2,128)(2,1)}, u32[]{:S(2)}, u32[]{:S(2)}) async-start(bf16[8,2,8,13824]{3,1,0,2:T(2,128)(2,1)} %bitcast.31), calls=%async_computation | async-start | bytes 7077888 | tf_op jit(solution)/shard_map/all_to_all | solution.py:20
  19.8 154.0 %all-reduce.8.cloned.1.call-start = ((), (), s32[]{:S(2)}) async-start(), calls=%async_computation.1 | async-start | bytes 2654208
  113.3 4.5 %copy-start.2 = (u32[32]{0:T(128)S(1)}, u32[32]{0:T(128)}, u32[]{:S(2)}) copy-start(u32[32]{0:T(128)} %constant.31) | copy-start | bytes 388
Sparse Core Ops, SparseCore 0:
  117.9 55.8 all-reduce.7
where the time goes:
time: 186 us; the launch traced here: 185 us
  blocking collectives  78.5 us (42%)
  waiting for transfers between devices  55.5 us (30%)
  between operations  14.8 us (8%)
  local copies, waits for them, and re-layouts  11.2 us (6%)
  other arithmetic  11 us (6%)
  matrix products  7.9 us (4%)
  starting transfers between devices  6.39 us (3%)
    unnamed x1, blocking collectives  78.5 us
    unnamed x2, waiting for transfers between devices  55.5 us
    mul x1, other arithmetic, per_device(): weighted = weight[:, None, :] * got_data  6.44 us
    all_to_all x1, starting transfers between devices, per_device(): lax.all_to_all(parts_four, 'dom', split_axis=2, concat_axis=0, tiled=True)  6.35 us
    reshape x1, local copies, waits for them, and re-layouts, per_device(): parts_four = particles.reshape(p_dev, 2, n_dom, shard_len)  6.24 us
  transfers between devices with their start and end apart: 2, of which 1 were waited for; matrix products, arithmetic and copies ran while one was open for 5% of the time, Pallas kernels for 0%

commit v1 on v0

v1 whole, which is shorter than its diff:
```python
import functools

import jax
import jax.numpy as jnp
from jax import lax
from jax.experimental import pallas as pl
from jax.experimental.pallas import tpu as pltpu
from jax.sharding import PartitionSpec as P

MESH = pl.DeviceIdType.MESH
LANES = 128
TILE_CAP = 1536
WIRE = jnp.float32


def tile_of(length):
    best = LANES
    for size in range(LANES, TILE_CAP + 1, LANES):
        if length % size == 0:
            best = size
    return best


def split2(value):
    high = value.astype(jnp.bfloat16)
    low = (value - high.astype(jnp.float32)).astype(jnp.bfloat16)
    return high, low


def dot2(left, value):
    high, low = split2(value)
    return jnp.dot(left, high, preferred_element_type=jnp.float32) + jnp.dot(
        left, low, preferred_element_type=jnp.float32
    )


def kernel(
    n_z, shard, rows, group_rows, wedges,
    x_ref, table_ref, aux_ref, avg_ref, total_ref,
    x_own, x_peer, aux_peer, table, sums, r1, mid, r2, last, rz,
    load_sem, pair_send, pair_recv, aux_send, aux_recv,
    s1_send, s1_recv, s2_send, s2_recv, z_send, z_recv,
):
    cls = lax.axis_index("cls")
    dom = lax.axis_index("dom")
    z = dom // 2
    core = lax.rem(dom, 2)
    peer = dom + 1 - 2 * core
    bit0 = lax.rem(cls, 2)
    bit1 = cls // 2
    near = cls + 1 - 2 * bit0
    far = cls + 2 - 4 * bit1
    both = near + 2 - 4 * bit1
    tile = tile_of(shard)

    def place(step):
        return lax.rem(z + 1 + step, n_z)

    loads = []
    for step in range(n_z):
        here = place(step) * 2 + core
        span = pl.ds(pl.multiple_of(here * shard, LANES), shard)
        one = pltpu.make_async_copy(x_ref.at[:, span], x_own.at[step], load_sem.at[step, 0])
        two = pltpu.make_async_copy(table_ref.at[:, span], table.at[step], load_sem.at[step, 1])
        one.start()
        two.start()
        loads.append((one, two))

    barrier = pltpu.get_barrier_semaphore()
    pl.semaphore_signal(barrier, inc=1, device_id={"dom": peer}, device_id_type=MESH)
    pl.semaphore_signal(barrier, inc=1, device_id={"cls": near}, device_id_type=MESH)
    pl.semaphore_signal(barrier, inc=1, device_id={"cls": far}, device_id_type=MESH)
    for step in range(n_z - 1):
        pl.semaphore_signal(
            barrier, inc=1, device_id={"dom": place(step) * 2 + core}, device_id_type=MESH
        )
    pl.semaphore_wait(barrier, n_z + 2)

    aux_copy = pltpu.make_async_remote_copy(
        src_ref=aux_ref, dst_ref=aux_peer, send_sem=aux_send, recv_sem=aux_recv,
        device_id={"dom": peer}, device_id_type=MESH,
    )
    aux_copy.start()
    pair = []
    for step in range(n_z):
        there = place(step) * 2 + (1 - core)
        span = pl.ds(pl.multiple_of(there * shard, LANES), shard)
        copy = pltpu.make_async_remote_copy(
            src_ref=x_ref.at[:, span], dst_ref=x_peer.at[step],
            send_sem=pair_send.at[step], recv_sem=pair_recv.at[step],
            device_id={"dom": peer}, device_id_type=MESH,
        )
        copy.start()
        pair.append(copy)
    aux_copy.wait()

    pick_own = aux_ref[0]
    pick_peer = aux_peer[0]
    pick_own_b = pick_own[:, :wedges].astype(jnp.bfloat16)
    pick_peer_b = pick_peer[:, :wedges].astype(jnp.bfloat16)
    member_own = aux_ref[1][:, :rows].astype(jnp.bfloat16)
    member_peer = aux_peer[1][:, :rows].astype(jnp.bfloat16)
    counts = jnp.dot(
        member_own, pick_own.astype(jnp.bfloat16), preferred_element_type=jnp.float32
    ) + jnp.dot(member_peer, pick_peer.astype(jnp.bfloat16), preferred_element_type=jnp.float32)
    n_groups = sums.shape[1]
    long = shard + LANES

    first, second, third = {}, {}, {}

    def compute(step):
        for copy in loads[step]:
            copy.wait()
        pair[step].wait()
        for group in range(n_groups):
            sums[step, group, :, pl.ds(shard, LANES)] = counts[
                group * group_rows : (group + 1) * group_rows
            ].astype(sums.dtype)

        @pl.loop(0, shard // tile)
        def _(index):
            span = pl.ds(pl.multiple_of(index * tile, LANES), tile)
            high, low = split2(table[step, :, span])
            total = None
            for pick, member, source in (
                (pick_own_b, member_own, x_own),
                (pick_peer_b, member_peer, x_peer),
            ):
                weight = jnp.dot(pick, high, preferred_element_type=jnp.float32) + jnp.dot(
                    pick, low, preferred_element_type=jnp.float32
                )
                part = dot2(member, weight * source[step, :, span].astype(jnp.float32))
                total = part if total is None else total + part
            for group in range(n_groups):
                sums[step, group, :, span] = total[
                    group * group_rows : (group + 1) * group_rows
                ].astype(sums.dtype)

        partner, other = (near, far) if step % 2 == 0 else (far, near)
        copies = []
        for slot, group in ((1, both), (0, partner)):
            copy = pltpu.make_async_remote_copy(
                src_ref=sums.at[step, group], dst_ref=r1.at[step, slot],
                send_sem=s1_send.at[step, slot], recv_sem=s1_recv.at[step, slot],
                device_id={"cls": partner}, device_id_type=MESH,
            )
            copy.start()
            copies.append(copy)
        first[step] = copies

    def forward(step):
        partner, other = (near, far) if step % 2 == 0 else (far, near)
        first[step][0].wait()
        mid[step] = (
            sums[step, other].astype(jnp.float32) + r1[step, 1].astype(jnp.float32)
        ).astype(mid.dtype)
        copy = pltpu.make_async_remote_copy(
            src_ref=mid.at[step], dst_ref=r2.at[step],
            send_sem=s2_send.at[step], recv_sem=s2_recv.at[step],
            device_id={"cls": other}, device_id_type=MESH,
        )
        copy.start()
        second[step] = copy

    def settle(step):
        first[step][1].wait()
        second[step].wait()
        last[step] = (
            sums[step, cls].astype(jnp.float32)
            + r1[step, 0].astype(jnp.float32)
            + r2[step].astype(jnp.float32)
        ).astype(last.dtype)
        if step < n_z - 1:
            copy = pltpu.make_async_remote_copy(
                src_ref=last.at[step], dst_ref=rz.at[step],
                send_sem=z_send.at[step], recv_sem=z_recv.at[step],
                device_id={"dom": place(step) * 2 + core}, device_id_type=MESH,
            )
            copy.start()
            third[step] = copy

    for step in range(n_z):
        compute(step)
        if step >= 2:
            forward(step - 2)
    for step in range(max(n_z - 2, 0), n_z):
        forward(step)
        settle(step - 2) if step >= 2 else None
    for step in range(n_z):
        if step not in third and not (max(n_z - 2, 0) <= step + 2 < n_z):
            settle(step)
    for step in range(n_z - 1):
        third[step].wait()

    tally = last[n_z - 1, :, pl.ds(shard, LANES)].astype(jnp.float32)
    for step in range(n_z - 1):
        tally = tally + rz[step, :, pl.ds(shard, LANES)].astype(jnp.float32)
    tally = tally[:, :wedges]

    @pl.loop(0, shard // tile)
    def _(index):
        span = pl.ds(pl.multiple_of(index * tile, LANES), tile)
        value = last[n_z - 1, :, span].astype(jnp.float32)
        for step in range(n_z - 1):
            value = value + rz[step, :, span].astype(jnp.float32)
        weight = table[n_z - 1, :, span]
        total = jnp.dot(
            tally, weight * weight,
            precision=lax.Precision.HIGHEST, preferred_element_type=jnp.float32,
        )
        mean = value / (total + 1.0)
        for index_k in range(group_rows // 2):
            avg_ref[index_k, :, span] = mean[2 * index_k : 2 * index_k + 2]
            total_ref[pl.ds(index_k, 1), span] = total[2 * index_k : 2 * index_k + 1]


def per_device(classes, particles, labels, wedge_index, wedge_table):
    n_cls = lax.axis_size("cls")
    n_dom = lax.axis_size("dom")
    p_dev, _, voxels = particles.shape
    wedges = wedge_table.shape[0]
    shard = voxels // n_dom
    n_z = n_dom // 2
    group = classes // n_cls
    rows = 2 * p_dev
    all_rows = 2 * classes
    flat = particles.reshape(rows, voxels)
    row = jnp.arange(rows, dtype=jnp.int32)
    lane = jnp.arange(LANES, dtype=jnp.int32)
    out_row = jnp.arange(all_rows, dtype=jnp.int32)
    wedge_row = jnp.repeat(wedge_index, 2)
    label_lane = jnp.pad(jnp.repeat(labels[:, 0], 2), (0, LANES - rows), constant_values=-1)
    pick = (wedge_row[:, None] == lane[None, :]).astype(jnp.float32)
    member = (
        (label_lane[None, :] == out_row[:, None] // 2)
        & (lane[None, :] % 2 == out_row[:, None] % 2)
    ).astype(jnp.float32)
    aux = jnp.stack([pick, member])
    long = shard + LANES
    any_space = pl.BlockSpec(memory_space=pl.ANY)
    vmem = pl.BlockSpec(memory_space=pltpu.VMEM)
    dma = pltpu.SemaphoreType.DMA
    return pl.pallas_call(
        functools.partial(kernel, n_z, shard, rows, 2 * group, wedges),
        out_shape=(
            jax.ShapeDtypeStruct((group, 2, shard), jnp.float32),
            jax.ShapeDtypeStruct((group, shard), jnp.float32),
        ),
        in_specs=[any_space, any_space, vmem],
        out_specs=(vmem, vmem),
        scratch_shapes=[
            pltpu.VMEM((n_z, rows, shard), jnp.bfloat16),
            pltpu.VMEM((n_z, rows, shard), jnp.bfloat16),
            pltpu.VMEM((2, rows, LANES), jnp.float32),
            pltpu.VMEM((n_z, wedges, shard), jnp.float32),
            pltpu.VMEM((n_z, n_cls, 2 * group, long), WIRE),
            pltpu.VMEM((n_z, 2, 2 * group, long), WIRE),
            pltpu.VMEM((n_z, 2 * group, long), WIRE),
            pltpu.VMEM((n_z, 2 * group, long), WIRE),
            pltpu.VMEM((n_z, 2 * group, long), WIRE),
            pltpu.VMEM((n_z, 2 * group, long), WIRE),
            dma((n_z, 2)), dma((n_z,)), dma((n_z,)), dma, dma,
            dma((n_z, 2)), dma((n_z, 2)), dma((n_z,)), dma((n_z,)),
            dma((n_z,)), dma((n_z,)),
        ],
        compiler_params=pltpu.CompilerParams(
            collective_id=0, has_side_effects=True, vmem_limit_bytes=60 * 1024 * 1024
        ),
    )(flat, wedge_table, aux)


CLASSES_PER_GROUP = 2


def solution(mesh):
    classes = CLASSES_PER_GROUP * mesh.shape["cls"]
    return jax.shard_map(
        functools.partial(per_device, classes),
        mesh=mesh,
        in_specs=(P(("cls", "dom"), None, None), P(("cls", "dom"), None), P(("cls", "dom")), P()),
        out_specs=(P("cls", None, "dom"), P("cls", "dom")),
        check_vma=False,
    )
```

time: 186 us -> 68.4 us (0.37)
  blocking collectives: 78.5 us -> 0 us
  Pallas kernels: 0 us -> 57.8 us
  waiting for transfers between devices: 55.5 us -> 0 us
  between operations: 14.8 us -> 0.66 us
  other arithmetic: 11 us -> 0.78 us
  matrix products: 7.9 us -> 0 us
  starting transfers between devices: 6.39 us -> 0 us
  local copies, waits for them, and re-layouts: 11.2 us -> 8.85 us
    unnamed x1 -> x0, blocking collectives: 78.5 us -> none
    pallas_call x0 -> x1, Pallas kernels: none -> 57.8 us  [per_device(): pl.pallas_call(functools.partial(kernel, n_z, shard, rows, 2 * group, wed...]
    unnamed x2 -> x0, waiting for transfers between devices: 55.5 us -> none
    dot_general x3 -> x0, matrix products: 7.9 us -> none  [the longest x1 3.06 us: per_device(): jnp.einsum('kp,pcv->kcv', member, weighted, precision=lax.Precision.HIGHEST)]
    mul x1 -> x0, other arithmetic: 6.44 us -> none  [per_device(): weighted = weight[:, None, :] * got_data]
    all_to_all x1 -> x0, starting transfers between devices: 6.35 us -> none  [per_device(): lax.all_to_all(parts_four, 'dom', split_axis=2, concat_axis=0, tiled=True)]
    reshape x2, local copies, waits for them, and re-layouts: 8.26 us -> 4.13 us  [the longest x1 4.05 us: per_device(): flat = particles.reshape(rows, voxels)]
    div x1 -> x0, other arithmetic: 2.35 us -> none  [per_device(): class_average = weighted_sum / (weight_total[:, None, :] + 1.0)]
  transfers between devices with their start and end apart: 2 -> 0, of which waited for: 1 -> 0; matrix products, arithmetic and copies ran while one was open for 5% -> 0% of each run, Pallas kernels for 0% -> 0%
where the time goes in v1:
time: 68.4 us; the launch traced here: 68.1 us
  Pallas kernels  57.8 us (85%)
  local copies, waits for them, and re-layouts  8.85 us (13%)
  other arithmetic  0.78 us (1%)
    pallas_call x1, Pallas kernels, per_device(): pl.pallas_call(functools.partial(kernel, n_z, shard, rows, 2 * group, wed...  57.8 us
    reshape x1, local copies, waits for them, and re-layouts, per_device(): flat = particles.reshape(rows, voxels)  4.05 us
    unnamed x2, local copies, waits for them, and re-layouts  3.18 us

profile of v1, /device:TPU:0, one launch (start us, length us, event | category | flops | bytes accessed | tf_op | source)
XLA Modules:
  0.0 68.1 jit_solution(13283842733947688092)
XLA Ops:
  0.6 0.7 %broadcast_in_dim.5 = s32[8,2]{1,0:T(8,128)S(1)} broadcast(s32[8]{0:T(128)} %bitcast.1), dimensions={0} | broadcast | bytes 96 | tf_op jit(solution)/shard_map/broadcast_in_dim | solution.py:232
  1.4 0.1 reshape.213
  1.5 0.1 compare_and_fusion
  1.5 0.7 %broadcast_in_dim.4 = s32[8,2]{1,0:T(8,128)S(1)} broadcast(s32[8]{0:T(128)} %param.6), dimensions={0} | broadcast | bytes 96 | tf_op jit(solution)/shard_map/broadcast_in_dim | solution.py:231
  2.3 0.1 eq.66
  2.4 0.1 iota_compare_fusion
  2.4 0.6 add_convert_fusion.aux_ref
  3.0 4.0 %reshape.212.x_ref = bf16[16,110592]{1,0:T(8,128)(2,1)} reshape(bf16[8,2,110592]{2,1,0:T(2,128)(2,1)} %param.4) | data formatting | bytes 7077888 | tf_op jit(solution)/shard_map/reshape | solution.py:227
  7.1 57.8 %shard_map.59 = (f32[2,2,13824]{2,1,0:T(2,128)}, f32[2,13824]{1,0:T(2,128)}) custom-call(bf16[16,110592]{1,0:T(8,128)(2,1)} %reshape.212.x_ref, f32[12,110592]{1,0:T(8,128)} %table_ref.1, f32[2,16,128]{2,1,0:T(8,128)} %add_convert_fusion.aux_ref), custom_call_target="tpu_custom_call" | custom-call | tf_op jit(solution)/shard_map/pallas_call | solution.py:243
  64.9 1.6 %copy.8 = f32[2,2,13824]{2,1,0:T(2,128)} copy(f32[2,2,13824]{2,1,0:T(2,128)} %get-tuple-element.6) | data formatting | bytes 442368
  66.5 1.5 %copy.9 = f32[2,13824]{1,0:T(2,128)} copy(f32[2,13824]{1,0:T(2,128)} %get-tuple-element.7) | data formatting | bytes 221184
  (3 shorter events, 0.0 us)

commit v2 on v0

v2 whole, which is shorter than its diff:
```python
import functools

import jax
import jax.numpy as jnp
from jax import lax
from jax.experimental import pallas as pl
from jax.experimental.pallas import tpu as pltpu
from jax.sharding import PartitionSpec as P

MESH = pl.DeviceIdType.MESH
LANES = 128
LEVELS = 32767.0
CLASSES_PER_GROUP = 2


def divisor(number, cap):
    return max(size for size in range(1, cap + 1) if number % size == 0)


def split2(value):
    high = value.astype(jnp.bfloat16)
    low = (value - high.astype(jnp.float32)).astype(jnp.bfloat16)
    return high, low


def dot(left, right):
    return jnp.dot(left, right, preferred_element_type=jnp.float32)


def spans_of(start, tiles, cap):
    unit = divisor(tiles, cap)

    def span(index, base=start):
        return pl.ds(pl.multiple_of(base + index * (unit * LANES), LANES), unit * LANES)

    return tiles // unit, unit, span


def encode(read, tiles, start, code_ref, scale_ref):
    turns, unit, span = spans_of(0, tiles, 9)

    def largest(index, top):
        block = jnp.abs(read(span(index, start)))
        for k in range(unit):
            top = jnp.maximum(top, block[:, k * LANES : (k + 1) * LANES])
        return top

    rows = code_ref.shape[0]
    top = lax.fori_loop(0, turns, largest, jnp.zeros((rows, LANES), jnp.float32))
    top = jnp.maximum(top, 1e-30)
    scale_ref[...] = top * (1.0 / LEVELS)
    factor = jnp.concatenate([LEVELS / top] * unit, axis=1)

    def store(index, carry):
        block = read(span(index, start)) * factor
        code_ref[:, span(index)] = jnp.round(block).astype(jnp.int32).astype(jnp.int16)
        return carry

    lax.fori_loop(0, turns, store, 0)


def decoder(code_ref, scale_ref, start, tiles):
    unit = divisor(tiles, 9)
    scale = jnp.concatenate([scale_ref[...]] * unit, axis=1)

    def read(span):
        here = pl.ds(pl.multiple_of(span.start - start, LANES), span.size)
        return code_ref[:, here].astype(jnp.int32).astype(jnp.float32) * scale

    return read


def kernel(
    n_z, shard, p_dev, group_rows, wedges, cuts,
    labels_ref, wedge_ref, x_ref, table_ref, mean_ref, total_ref,
    x_own, x_peer, aux_own, aux_peer, table, sums, last, tallies,
    load_sem, table_sem, pair_send, pair_recv, aux_send, aux_recv,
    *parts_refs,
):
    cls = lax.axis_index("cls")
    dom = lax.axis_index("dom")
    z = dom // 2
    core = lax.rem(dom, 2)
    peer = dom + 1 - 2 * core
    near = cls + 1 - 2 * lax.rem(cls, 2)
    far = cls + 2 - 4 * (cls // 2)
    both = near + 2 - 4 * (cls // 2)
    n_groups = sums.shape[1]
    rows = 2 * p_dev
    each = len(parts_refs) // len(cuts)
    bufs = [parts_refs[i * each : (i + 1) * each] for i in range(len(cuts))]

    def place(step):
        return lax.rem(z + 1 + step, n_z)

    loads = []
    for step in range(n_z):
        here = place(step) * 2 + core
        span = pl.ds(pl.multiple_of(here * shard, LANES), shard)
        copies = [pltpu.make_async_copy(table_ref.at[:, span], table.at[step], table_sem.at[step])]
        for p in range(p_dev):
            copies.append(
                pltpu.make_async_copy(
                    x_ref.at[p, :, span], x_own.at[step, pl.ds(2 * p, 2)], load_sem.at[step, p]
                )
            )
        for copy in copies:
            copy.start()
        loads.append(copies)

    barrier = pltpu.get_barrier_semaphore()
    pl.semaphore_signal(barrier, inc=1, device_id={"dom": peer}, device_id_type=MESH)
    pl.semaphore_signal(barrier, inc=1, device_id={"cls": near}, device_id_type=MESH)
    pl.semaphore_signal(barrier, inc=1, device_id={"cls": far}, device_id_type=MESH)
    for step in range(n_z - 1):
        pl.semaphore_signal(
            barrier, inc=1, device_id={"dom": place(step) * 2 + core}, device_id_type=MESH
        )

    row = lax.broadcasted_iota(jnp.int32, (rows, LANES), 0)
    lane = lax.broadcasted_iota(jnp.int32, (rows, LANES), 1)
    out_row = lax.broadcasted_iota(jnp.int32, (n_groups * group_rows, LANES), 0)
    out_lane = lax.broadcasted_iota(jnp.int32, (n_groups * group_rows, LANES), 1)
    wedge_of = jnp.zeros((rows, LANES), jnp.int32)
    label_of = jnp.zeros_like(out_row) - 1
    for p in range(p_dev):
        wedge_of = jnp.where((row == 2 * p) | (row == 2 * p + 1), wedge_ref[p], wedge_of)
        label_of = jnp.where(
            (out_lane == 2 * p) | (out_lane == 2 * p + 1), labels_ref[p], label_of
        )
    aux_own[0] = (wedge_of == lane).astype(jnp.float32)
    aux_own[1] = (
        (out_row == 2 * label_of + (out_lane & 1)) & (label_of >= 0)
    ).astype(jnp.float32)

    pl.semaphore_wait(barrier, n_z + 2)

    pair = []
    for step in range(n_z):
        there = place(step) * 2 + (1 - core)
        span = pl.ds(pl.multiple_of(there * shard, LANES), shard)
        copies = []
        for p in range(p_dev):
            copy = pltpu.make_async_remote_copy(
                src_ref=x_ref.at[p, :, span], dst_ref=x_peer.at[step, pl.ds(2 * p, 2)],
                send_sem=pair_send.at[step, p], recv_sem=pair_recv.at[step, p],
                device_id={"dom": peer}, device_id_type=MESH,
            )
            copy.start()
            copies.append(copy)
        pair.append(copies)
    aux_copy = pltpu.make_async_remote_copy(
        src_ref=aux_own, dst_ref=aux_peer, send_sem=aux_send, recv_sem=aux_recv,
        device_id={"dom": peer}, device_id_type=MESH,
    )
    aux_copy.start()
    aux_copy.wait()

    pick_own = aux_own[0].astype(jnp.bfloat16)
    pick_peer = aux_peer[0].astype(jnp.bfloat16)
    member_own = aux_own[1][:, :rows].astype(jnp.bfloat16)
    member_peer = aux_peer[1][:, :rows].astype(jnp.bfloat16)
    counts = dot(member_own, pick_own) + dot(member_peer, pick_peer)
    for group in range(n_groups):
        tallies[group] = counts[group * group_rows : (group + 1) * group_rows]
    pick_own = pick_own[:, :wedges]
    pick_peer = pick_peer[:, :wedges]

    def send(source, target, sems, slot, who):
        copy = pltpu.make_async_remote_copy(
            src_ref=source, dst_ref=target, send_sem=sems[0].at[slot], recv_sem=sems[1].at[slot],
            device_id=who, device_id_type=MESH,
        )
        copy.start()
        return copy

    first, second, third = {}, {}, {}

    def compute(step, part):
        start, tiles = cuts[part]
        (q1, c1, r1, d1, q2, c2, r2, d2, q3, c3, r3, d3, sa, sb, ra, rb) = bufs[part]
        if part == 0:
            for copy in loads[step] + pair[step]:
                copy.wait()
        turns, unit, span_of = spans_of(start, tiles, 12)

        @pl.loop(0, turns)
        def _(index):
            span = span_of(index)
            high, low = split2(table[step, :, span])
            total = None
            for pick, member, source in (
                (pick_own, member_own, x_own),
                (pick_peer, member_peer, x_peer),
            ):
                weight = dot(pick, high) + dot(pick, low)
                up, down = split2(weight * source[step, :, span].astype(jnp.float32))
                piece = dot(member, up) + dot(member, down)
                total = piece if total is None else total + piece
            for group in range(n_groups):
                sums[step, group, :, span] = total[group * group_rows : (group + 1) * group_rows]

        partner = near if part == 0 else far
        copies = []
        for slot, group in ((1, both), (0, partner)):
            encode(
                lambda span: sums[step, group, :, span], tiles, start,
                q1.at[step, slot], c1.at[step, slot, :, pl.ds(0, LANES)],
            )
            if part == 0:
                c1[step, slot, :, pl.ds(LANES, LANES)] = tallies[group]
            for kind, source, target in ((0, c1, d1), (1, q1, r1)):
                copies.append(
                    send(
                        source.at[step, slot], target.at[step, slot], (sa, ra),
                        4 * step + 2 * slot + kind, {"cls": partner},
                    )
                )
        first[step, part] = copies

    def forward(step, part):
        start, tiles = cuts[part]
        (q1, c1, r1, d1, q2, c2, r2, d2, q3, c3, r3, d3, sa, sb, ra, rb) = bufs[part]
        other = far if part == 0 else near
        for copy in first[step, part][:2]:
            copy.wait()
        got = decoder(r1.at[step, 1], d1.at[step, 1, :, pl.ds(0, LANES)], start, tiles)
        encode(
            lambda span: sums[step, other, :, span] + got(span), tiles, start,
            q2.at[step], c2.at[step, :, pl.ds(0, LANES)],
        )
        if part == 0:
            c2[step, :, pl.ds(LANES, LANES)] = tallies[other] + d1[step, 1, :, pl.ds(LANES, LANES)]
        second[step, part] = [
            send(source.at[step], target.at[step], (sb, rb), 4 * step + kind, {"cls": other})
            for kind, source, target in ((0, c2, d2), (1, q2, r2))
        ]

    def settle(step, part):
        start, tiles = cuts[part]
        (q1, c1, r1, d1, q2, c2, r2, d2, q3, c3, r3, d3, sa, sb, ra, rb) = bufs[part]
        for copy in first[step, part][2:] + second[step, part]:
            copy.wait()
        got1 = decoder(r1.at[step, 0], d1.at[step, 0, :, pl.ds(0, LANES)], start, tiles)
        got2 = decoder(r2.at[step], d2.at[step, :, pl.ds(0, LANES)], start, tiles)

        def read(span):
            return sums[step, cls, :, span] + got1(span) + got2(span)

        tally = None
        if part == 0:
            tally = (
                tallies[cls]
                + d1[step, 0, :, pl.ds(LANES, LANES)]
                + d2[step, :, pl.ds(LANES, LANES)]
            )
        if step == n_z - 1:
            turns, _, span_of = spans_of(start, tiles, 9)

            @pl.loop(0, turns)
            def _(index):
                span = span_of(index)
                last[:, span] = read(span)

            return tally
        encode(read, tiles, start, q3.at[step], c3.at[step, :, pl.ds(0, LANES)])
        if part == 0:
            c3[step, :, pl.ds(LANES, LANES)] = tally
        there = place(step) * 2 + core
        third[step, part] = [
            send(source.at[step], target.at[step], (sb, rb), 4 * step + 2 + kind, {"dom": there})
            for kind, source, target in ((0, c3, d3), (1, q3, r3))
        ]
        return None

    n_parts = len(cuts)
    units = [(step, part) for step in range(n_z) for part in range(n_parts)]
    tally = None
    for turn in range(len(units) + 4):
        if turn < len(units):
            compute(*units[turn])
        if 2 <= turn < len(units) + 2:
            forward(*units[turn - 2])
        if 4 <= turn:
            found = settle(*units[turn - 4])
            tally = found if found is not None else tally

    for part in range(n_parts):
        start, tiles = cuts[part]
        (q1, c1, r1, d1, q2, c2, r2, d2, q3, c3, r3, d3, sa, sb, ra, rb) = bufs[part]
        for step in range(n_z - 1):
            for copy in third[step, part]:
                copy.wait()
        if part == 0:
            for step in range(n_z - 1):
                tally = tally + d3[step, :, pl.ds(LANES, LANES)]
            tally = tally[:, :wedges]
        got = [
            decoder(r3.at[step], d3.at[step, :, pl.ds(0, LANES)], start, tiles)
            for step in range(n_z - 1)
        ]
        turns, _, span_of = spans_of(start, tiles, 9)

        @pl.loop(0, turns)
        def _(index):
            span = span_of(index)
            value = last[:, span]
            for read in got:
                value = value + read(span)
            weight = table[n_z - 1, :, span]
            total = jnp.dot(
                tally, weight * weight,
                precision=lax.Precision.HIGHEST, preferred_element_type=jnp.float32,
            )
            mean_ref[:, span] = value / (total + 1.0)
            total_ref[:, span] = total


def finish(mean_ref, total_ref, avg_out, total_out):
    for index in range(avg_out.shape[0]):
        avg_out[index] = mean_ref[pl.ds(2 * index, 2)]
        total_out[pl.ds(index, 1)] = total_ref[pl.ds(2 * index, 1)]


def per_device(classes, particles, labels, wedge_index, wedge_table):
    n_cls = lax.axis_size("cls")
    n_dom = lax.axis_size("dom")
    p_dev, _, voxels = particles.shape
    wedges = wedge_table.shape[0]
    shard = voxels // n_dom
    n_z = n_dom // 2
    group = classes // n_cls
    rows = 2 * p_dev
    out_rows = 2 * group
    tiles = shard // LANES
    cuts = ((0, tiles // 2), (tiles // 2 * LANES, tiles - tiles // 2))
    any_space = pl.BlockSpec(memory_space=pl.ANY)
    vmem = pl.BlockSpec(memory_space=pltpu.VMEM)
    smem = pl.BlockSpec(memory_space=pltpu.SMEM)
    dma = pltpu.SemaphoreType.DMA
    scratch = [
        pltpu.VMEM((n_z, rows, shard), jnp.bfloat16),
        pltpu.VMEM((n_z, rows, shard), jnp.bfloat16),
        pltpu.VMEM((2, rows, LANES), jnp.float32),
        pltpu.VMEM((2, rows, LANES), jnp.float32),
        pltpu.VMEM((n_z, wedges, shard), jnp.float32),
        pltpu.VMEM((n_z, n_cls, out_rows, shard), jnp.float32),
        pltpu.VMEM((out_rows, shard), jnp.float32),
        pltpu.VMEM((n_cls, out_rows, LANES), jnp.float32),
        dma((n_z, p_dev)), dma((n_z,)), dma((n_z, p_dev)), dma((n_z, p_dev)), dma, dma,
    ]
    for part, (_, count) in enumerate(cuts):
        wide = LANES * (2 if part == 0 else 1)
        for lead in ((n_z, 2), (n_z,), (n_z,)):
            for _ in range(2):
                scratch.append(pltpu.VMEM((*lead, out_rows, count * LANES), jnp.int16))
                scratch.append(pltpu.VMEM((*lead, out_rows, wide), jnp.float32))
        scratch += [dma((4 * n_z,)) for _ in range(4)]
    mean, total = pl.pallas_call(
        functools.partial(kernel, n_z, shard, p_dev, out_rows, wedges, cuts),
        out_shape=(
            jax.ShapeDtypeStruct((out_rows, shard), jnp.float32),
            jax.ShapeDtypeStruct((out_rows, shard), jnp.float32),
        ),
        in_specs=[smem, smem, any_space, any_space],
        out_specs=(vmem, vmem),
        scratch_shapes=scratch,
        compiler_params=pltpu.CompilerParams(
            collective_id=0, has_side_effects=True, vmem_limit_bytes=60 * 1024 * 1024
        ),
    )(labels.reshape(p_dev), wedge_index, particles, wedge_table)
    return pl.pallas_call(
        finish,
        out_shape=(
            jax.ShapeDtypeStruct((group, 2, shard), jnp.float32),
            jax.ShapeDtypeStruct((group, shard), jnp.float32),
        ),
        in_specs=[vmem, vmem],
        out_specs=(vmem, vmem),
    )(mean, total)


def solution(mesh):
    classes = CLASSES_PER_GROUP * mesh.shape["cls"]
    return jax.shard_map(
        functools.partial(per_device, classes),
        mesh=mesh,
        in_specs=(P(("cls", "dom"), None, None), P(("cls", "dom"), None), P(("cls", "dom")), P()),
        out_specs=(P("cls", None, "dom"), P("cls", "dom")),
        check_vma=False,
    )
```

time: 186 us -> 52.6 us (0.28)
  blocking collectives: 78.5 us -> 0 us
  waiting for transfers between devices: 55.5 us -> 0 us
  Pallas kernels: 0 us -> 51.8 us
  between operations: 14.8 us -> 0.64 us
  local copies, waits for them, and re-layouts: 11.2 us -> 0 us
  other arithmetic: 11 us -> 0 us
  matrix products: 7.9 us -> 0 us
  starting transfers between devices: 6.39 us -> 0 us
    unnamed x1 -> x0, blocking collectives: 78.5 us -> none
    unnamed x2 -> x0, waiting for transfers between devices: 55.5 us -> none
    pallas_call x0 -> x2, Pallas kernels: none -> 51.8 us  [the longest x1 50 us: per_device(): pl.pallas_call(functools.partial(kernel, n_z, shard, p_dev, out_rows, wed...]
    reshape x2 -> x0, local copies, waits for them, and re-layouts: 8.26 us -> none  [the longest x1 6.24 us: per_device(): parts_four = particles.reshape(p_dev, 2, n_dom, shard_len)]
    dot_general x3 -> x0, matrix products: 7.9 us -> none  [the longest x1 3.06 us: per_device(): jnp.einsum('kp,pcv->kcv', member, weighted, precision=lax.Precision.HIGHEST)]
    mul x1 -> x0, other arithmetic: 6.44 us -> none  [per_device(): weighted = weight[:, None, :] * got_data]
    all_to_all x1 -> x0, starting transfers between devices: 6.35 us -> none  [per_device(): lax.all_to_all(parts_four, 'dom', split_axis=2, concat_axis=0, tiled=True)]
    div x1 -> x0, other arithmetic: 2.35 us -> none  [per_device(): class_average = weighted_sum / (weight_total[:, None, :] + 1.0)]
  transfers between devices with their start and end apart: 2 -> 0, of which waited for: 1 -> 0; matrix products, arithmetic and copies ran while one was open for 5% -> 0% of each run, Pallas kernels for 0% -> 0%
where the time goes in v2:
time: 52.6 us; the launch traced here: 52.4 us
  Pallas kernels  51.8 us (98%)
  between operations  0.64 us (1%)
    pallas_call x1, Pallas kernels, per_device(): pl.pallas_call(functools.partial(kernel, n_z, shard, p_dev, out_rows, wed...  50 us
    pallas_call x1, Pallas kernels, per_device(): pl.pallas_call(finish, out_shape=(jax.ShapeDtypeStruct((group, 2, shard),...  1.8 us

profile of v2, /device:TPU:0, one launch (start us, length us, event | category | flops | bytes accessed | tf_op | source)
XLA Modules:
  0.0 52.4 jit_solution(7827352705027344578)
XLA Ops:
  0.6 50.0 %shard_map.59 = (f32[4,13824]{1,0:T(4,128)}, f32[4,13824]{1,0:T(4,128)}) custom-call(s32[8]{0:T(128)} %bitcast.1, s32[8]{0:T(128)} %wedge_ref.1, bf16[8,2,110592]{2,1,0:T(2,128)(2,1)} %x_ref.1, f32[12,110592]{1,0:T(8,128)} %table_ref.1), custom_call_target="tpu_custom_call" | custom-call | tf_op jit(solution)/shard_map/pallas_call | solution.py:359
  50.6 1.8 %shard_map.60 = (f32[2,2,13824]{2,1,0:T(2,128)}, f32[2,13824]{1,0:T(2,128)}) custom-call(f32[4,13824]{1,0:T(4,128)} %get-tuple-element.4.mean_ref, f32[4,13824]{1,0:T(4,128)} %get-tuple-element.5.total_ref), custom_call_target="tpu_custom_call" | custom-call | tf_op jit(solution)/shard_map/pallas_call | solution.py:372

commit v3 on v2

--- a/solution.py
+++ b/solution.py
@@ -23,6 +23,11 @@
     return high, low
 
 
+def stack2(value):
+    high = value.astype(jnp.bfloat16).astype(jnp.float32)
+    return jnp.concatenate([high, value - high], axis=0).astype(jnp.bfloat16)
+
+
 def dot(left, right):
     return jnp.dot(left, right, preferred_element_type=jnp.float32)
 
@@ -73,7 +78,7 @@
 def kernel(
     n_z, shard, p_dev, group_rows, wedges, cuts,
     labels_ref, wedge_ref, x_ref, table_ref, mean_ref, total_ref,
-    x_own, x_peer, aux_own, aux_peer, table, sums, last, tallies,
+    x_all, aux_own, aux_peer, table, sums, last, tallies,
     load_sem, table_sem, pair_send, pair_recv, aux_send, aux_recv,
     *parts_refs,
 ):
@@ -101,7 +106,7 @@
         for p in range(p_dev):
             copies.append(
                 pltpu.make_async_copy(
-                    x_ref.at[p, :, span], x_own.at[step, pl.ds(2 * p, 2)], load_sem.at[step, p]
+                    x_ref.at[p, :, span], x_all.at[step, pl.ds(2 * p, 2)], load_sem.at[step, p]
                 )
             )
         for copy in copies:
@@ -142,7 +147,7 @@
         copies = []
         for p in range(p_dev):
             copy = pltpu.make_async_remote_copy(
-                src_ref=x_ref.at[p, :, span], dst_ref=x_peer.at[step, pl.ds(2 * p, 2)],
+                src_ref=x_ref.at[p, :, span], dst_ref=x_all.at[step, pl.ds(rows + 2 * p, 2)],
                 send_sem=pair_send.at[step, p], recv_sem=pair_recv.at[step, p],
                 device_id={"dom": peer}, device_id_type=MESH,
             )
@@ -163,8 +168,10 @@
     counts = dot(member_own, pick_own) + dot(member_peer, pick_peer)
     for group in range(n_groups):
         tallies[group] = counts[group * group_rows : (group + 1) * group_rows]
-    pick_own = pick_own[:, :wedges]
-    pick_peer = pick_peer[:, :wedges]
+    pick = jnp.concatenate([aux_own[0], aux_peer[0]], axis=0)[:, :wedges]
+    pick = jnp.concatenate([pick, pick], axis=1).astype(jnp.bfloat16)
+    member = jnp.concatenate([aux_own[1][:, :rows], aux_peer[1][:, :rows]] * 2, axis=1)
+    member = member.astype(jnp.bfloat16)
 
     def send(source, target, sems, slot, who):
         copy = pltpu.make_async_remote_copy(
@@ -187,16 +194,9 @@
         @pl.loop(0, turns)
         def _(index):
             span = span_of(index)
-            high, low = split2(table[step, :, span])
-            total = None
-            for pick, member, source in (
-                (pick_own, member_own, x_own),
-                (pick_peer, member_peer, x_peer),
-            ):
-                weight = dot(pick, high) + dot(pick, low)
-                up, down = split2(weight * source[step, :, span].astype(jnp.float32))
-                piece = dot(member, up) + dot(member, down)
-                total = piece if total is None else total + piece
+            weight = dot(pick, stack2(table[step, :, span]))
+            high, low = split2(weight * x_all[step, :, span].astype(jnp.float32))
+            total = dot(member, jnp.concatenate([high, low], axis=0))
             for group in range(n_groups):
                 sums[step, group, :, span] = total[group * group_rows : (group + 1) * group_rows]
 
@@ -294,7 +294,8 @@
         if part == 0:
             for step in range(n_z - 1):
                 tally = tally + d3[step, :, pl.ds(LANES, LANES)]
-            tally = tally[:, :wedges]
+            tally = stack2(tally[:, :wedges])
+            tally = jnp.concatenate([tally, tally], axis=1)
         got = [
             decoder(r3.at[step], d3.at[step, :, pl.ds(0, LANES)], start, tiles)
             for step in range(n_z - 1)
@@ -308,10 +309,8 @@
             for read in got:
                 value = value + read(span)
             weight = table[n_z - 1, :, span]
-            total = jnp.dot(
-                tally, weight * weight,
-                precision=lax.Precision.HIGHEST, preferred_element_type=jnp.float32,
-            )
+            total = dot(tally, stack2(weight * weight))
+            total = total[:group_rows] + total[group_rows:]
             mean_ref[:, span] = value / (total + 1.0)
             total_ref[:, span] = total
 
@@ -339,8 +338,7 @@
     smem = pl.BlockSpec(memory_space=pltpu.SMEM)
     dma = pltpu.SemaphoreType.DMA
     scratch = [
-        pltpu.VMEM((n_z, rows, shard), jnp.bfloat16),
-        pltpu.VMEM((n_z, rows, shard), jnp.bfloat16),
+        pltpu.VMEM((n_z, 2 * rows, shard), jnp.bfloat16),
         pltpu.VMEM((2, rows, LANES), jnp.float32),
         pltpu.VMEM((2, rows, LANES), jnp.float32),
         pltpu.VMEM((n_z, wedges, shard), jnp.float32),

time: 52.6 us -> 43 us (0.82)
  Pallas kernels: 51.8 us -> 42.1 us
    pallas_call x1, Pallas kernels: 50 us -> 40.3 us  [per_device(): pl.pallas_call(functools.partial(kernel, n_z, shard, p_dev, out_rows, wed...]
where the time goes in v3:
time: 43 us; the launch traced here: 42.8 us
  Pallas kernels  42.1 us (98%)
  between operations  0.64 us (1%)
    pallas_call x1, Pallas kernels, per_device(): pl.pallas_call(functools.partial(kernel, n_z, shard, p_dev, out_rows, wed...  40.3 us
    pallas_call x1, Pallas kernels, per_device(): pl.pallas_call(finish, out_shape=(jax.ShapeDtypeStruct((group, 2, shard),...  1.8 us

profile of v3, /device:TPU:0, one launch (start us, length us, event | category | flops | bytes accessed | tf_op | source)
XLA Modules:
  0.0 42.8 jit_solution(13380843717155602836)
XLA Ops:
  0.6 40.3 %shard_map.59 = (f32[4,13824]{1,0:T(4,128)}, f32[4,13824]{1,0:T(4,128)}) custom-call(s32[8]{0:T(128)} %bitcast.1, s32[8]{0:T(128)} %wedge_ref.1, bf16[8,2,110592]{2,1,0:T(2,128)(2,1)} %x_ref.1, f32[12,110592]{1,0:T(8,128)} %table_ref.1), custom_call_target="tpu_custom_call" | custom-call | tf_op jit(solution)/shard_map/pallas_call | solution.py:357
  41.0 1.8 %shard_map.60 = (f32[2,2,13824]{2,1,0:T(2,128)}, f32[2,13824]{1,0:T(2,128)}) custom-call(f32[4,13824]{1,0:T(4,128)} %get-tuple-element.4.mean_ref, f32[4,13824]{1,0:T(4,128)} %get-tuple-element.5.total_ref), custom_call_target="tpu_custom_call" | custom-call | tf_op jit(solution)/shard_map/pallas_call | solution.py:370
